TPU v7x, 32 devices: a whole 2x2x4 slice. The times are simulated.
32 devices in a mesh: dp: 8 (over y, x, core), tensor: 4 (over z).
Axes of the slice: x: 2, y: 2, z: 4, core: 2. Of those that a mesh axis runs over, the one named last changes fastest.
Arguments:
- tokens: bfloat16 [8192, 1280], P(('dp', 'tensor')), may hold values from -6 to 6
- w_query: bfloat16 [1280, 1280], P('dp', 'tensor'), may hold values from -0.15625 to 0.15625
- w_key: bfloat16 [1280, 1280], P('dp', 'tensor'), may hold values from -0.15625 to 0.15625
- w_value: bfloat16 [1280, 1280], P('dp', 'tensor'), may hold values from -0.15625 to 0.15625
- w_out: bfloat16 [1280, 1280], P('dp', 'tensor'), may hold values from -0.15625 to 0.15625
- w_up: bfloat16 [1280, 5120], P('dp', 'tensor'), may hold values from -0.15625 to 0.15625
- w_gate: bfloat16 [1280, 5120], P('dp', 'tensor'), may hold values from -0.15625 to 0.15625
- w_down: bfloat16 [1280, 5120], P('dp', 'tensor'), may hold values from -0.078125 to 0.078125
- qk_scale: float32 [1280], P('tensor'), may hold values from 0.8 to 1.8
- up_scale: float32 [5120], P('tensor'), may hold values from 0.5 to 2
- gate_scale: float32 [5120], P('tensor'), may hold values from 0.5 to 2
- alpha_attn: float32 [1280], replicated, may hold values from 0.2 to 0.6
- alpha_mlp: float32 [1280], replicated, may hold values from 0.2 to 0.6
- cotangent: bfloat16 [8192, 1280], P(('dp', 'tensor')), may hold values from -6 to 6
Outputs:
- output: bfloat16 [8192, 1280], P(('dp', 'tensor'))
- tokens_gradient: float32 [8192, 1280], P(('dp', 'tensor'))
- w_query_gradient: float32 [1280, 1280], P('dp', 'tensor')
- w_key_gradient: float32 [1280, 1280], P('dp', 'tensor')
- w_value_gradient: float32 [1280, 1280], P('dp', 'tensor')
- w_out_gradient: float32 [1280, 1280], P('dp', 'tensor')
- w_up_gradient: float32 [1280, 5120], P('dp', 'tensor')
- w_gate_gradient: float32 [1280, 5120], P('dp', 'tensor')
- w_down_gradient: float32 [1280, 5120], P('dp', 'tensor')
- qk_scale_gradient: float32 [1280], P('tensor')
- up_scale_gradient: float32 [5120], P('tensor')
- gate_scale_gradient: float32 [5120], P('tensor')
- alpha_attn_gradient: float32 [1280], replicated
- alpha_mlp_gradient: float32 [1280], replicated
All inputs are finite; a program needn't handle non-finite values.
Results may differ from a plain program's by a relative error of at most 0.017.
Values may be sent and summed in bfloat16 or wider, within the bound.
A program may use at most 192 MiB of HBM per device.

v0:
```python
import jax
import jax.numpy as jnp
from jax import lax
from jax.sharding import PartitionSpec as P

HEAD_DIM = 64
HIGH = lax.Precision.HIGHEST
EPS = 1e-06


def unit_rows(value):
    scale = lax.rsqrt(jnp.mean(value * value, axis=-1, keepdims=True) + EPS)
    return (value * scale, scale)


def unit_back(grad, unit, scale):
    return scale * (grad - unit * jnp.mean(grad * unit, axis=-1, keepdims=True))


def contract_rows(left, right):
    return lax.dot_general(
        left, right, (((0,), (0,)), ((), ())), preferred_element_type=jnp.float32
    )


def contract_cols(left, right):
    return lax.dot_general(
        left, right, (((1,), (1,)), ((), ())), preferred_element_type=jnp.float32
    )


def tables(width, length):
    half_dim = HEAD_DIM // 2
    column = lax.iota(jnp.int32, width)
    within = column % HEAD_DIM
    freq_index = (within % half_dim).astype(jnp.float32)
    frequency = 10000.0 ** (-freq_index / half_dim)
    position = lax.iota(jnp.float32, length)
    angle = position[:, None] * frequency[None, :]
    first_half = (within < half_dim)[None, :]
    heads = width // HEAD_DIM
    member = (
        lax.broadcasted_iota(jnp.int32, (width, heads), 0) // HEAD_DIM
        == lax.broadcasted_iota(jnp.int32, (width, heads), 1)
    ).astype(jnp.float32)
    return (jnp.cos(angle), jnp.sin(angle), first_half, member)


def rope_apply(value, cosine, sine, first_half):
    half_dim = HEAD_DIM // 2
    turned = jnp.where(
        first_half, -jnp.roll(value, -half_dim, axis=1), jnp.roll(value, half_dim, axis=1)
    )
    return value * cosine + turned * sine


def rope_back(grad, cosine, sine, first_half):
    half_dim = HEAD_DIM // 2
    weighted = grad * sine
    turned = jnp.where(
        first_half, jnp.roll(weighted, -half_dim, axis=1), -jnp.roll(weighted, half_dim, axis=1)
    )
    return grad * cosine + turned


def head_unit(value, member):
    mean_sq = (
        jnp.dot(value * value, member, precision=HIGH, preferred_element_type=jnp.float32)
        / HEAD_DIM
    )
    scale = jnp.dot(
        lax.rsqrt(mean_sq + EPS), member.T, precision=HIGH, preferred_element_type=jnp.float32
    )
    return (value * scale, scale)


def head_back(grad, unit, scale, member):
    inner = (
        jnp.dot(grad * unit, member, precision=HIGH, preferred_element_type=jnp.float32) / HEAD_DIM
    )
    spread = jnp.dot(inner, member.T, precision=HIGH, preferred_element_type=jnp.float32)
    return scale * (grad - unit * spread)


def block_scores(query3, key3, start, stop, block):
    scale = HEAD_DIM ** (-0.5)
    scores = (
        jnp.einsum(
            "qhd,khd->hqk", query3[start:stop], key3[:stop], preferred_element_type=jnp.float32
        )
        * scale
    )
    allowed = start + lax.broadcasted_iota(jnp.int32, (block, stop), 0) >= lax.broadcasted_iota(
        jnp.int32, (block, stop), 1
    )
    return jnp.where(allowed[None], scores, -jnp.inf)


def attend(query3, key3, value3, block):
    length = query3.shape[0]
    outputs = []
    totals = []
    for block_id in range(length // block):
        start = block_id * block
        stop = start + block
        scores = block_scores(query3, key3, start, stop, block)
        row_max = jnp.max(scores, axis=-1, keepdims=True)
        log_total = jnp.log(jnp.sum(jnp.exp(scores - row_max), axis=-1, keepdims=True)) + row_max
        weights = jnp.exp(scores - log_total).astype(jnp.bfloat16)
        outputs.append(
            jnp.einsum("hqk,khd->qhd", weights, value3[:stop], preferred_element_type=jnp.float32)
        )
        totals.append(log_total)
    return (jnp.concatenate(outputs, axis=0), totals)


def attend_back(query3, key3, value3, grad3, totals, block):
    length = query3.shape[0]
    scale = HEAD_DIM ** (-0.5)
    query_parts = []
    key_grad = jnp.zeros(key3.shape, jnp.float32)
    value_grad = jnp.zeros(value3.shape, jnp.float32)
    for block_id in range(length // block):
        start = block_id * block
        stop = start + block
        scores = block_scores(query3, key3, start, stop, block)
        probs = jnp.exp(scores - totals[block_id])
        g_probs = jnp.einsum(
            "qhd,khd->hqk", grad3[start:stop], value3[:stop], preferred_element_type=jnp.float32
        )
        inner = jnp.sum(probs * g_probs, axis=-1, keepdims=True)
        g_scores = (probs * (g_probs - inner)).astype(jnp.bfloat16)
        query_parts.append(
            jnp.einsum("hqk,khd->qhd", g_scores, key3[:stop], preferred_element_type=jnp.float32)
            * scale
        )
        key_grad = key_grad.at[:stop].add(
            jnp.einsum(
                "hqk,qhd->khd", g_scores, query3[start:stop], preferred_element_type=jnp.float32
            )
            * scale
        )
        value_grad = value_grad.at[:stop].add(
            jnp.einsum(
                "hqk,qhd->khd",
                probs.astype(jnp.bfloat16),
                grad3[start:stop],
                preferred_element_type=jnp.float32,
            )
        )
    return (jnp.concatenate(query_parts, axis=0), key_grad, value_grad)


def gather_attention(w_query, w_key, w_value, w_out):
    return (
        lax.all_gather(w_query, "dp", axis=0, tiled=True),
        lax.all_gather(w_key, "dp", axis=0, tiled=True),
        lax.all_gather(w_value, "dp", axis=0, tiled=True),
        lax.all_gather(w_out, "dp", axis=0, tiled=True),
    )


def gather_feedforward(w_up, w_gate, w_down):
    return (
        lax.all_gather(w_up, "dp", axis=0, tiled=True),
        lax.all_gather(w_gate, "dp", axis=0, tiled=True),
        lax.all_gather(w_down, "dp", axis=0, tiled=True),
    )


def on_device(
    tokens,
    w_query,
    w_key,
    w_value,
    w_out,
    w_up,
    w_gate,
    w_down,
    qk_scale,
    up_scale,
    gate_scale,
    alpha_attn,
    alpha_mlp,
    cotangent,
):
    query_w, key_w, value_w, out_w = gather_attention(w_query, w_key, w_value, w_out)
    whole = lax.all_gather(tokens, "tensor", axis=0, tiled=True)
    length = whole.shape[0]
    width = query_w.shape[1]
    block = min(512, length)
    cosine, sine, first_half, member = tables(width, length)
    shape3 = (length, width // HEAD_DIM, HEAD_DIM)
    q_raw = jnp.dot(whole, query_w, preferred_element_type=jnp.float32)
    k_raw = jnp.dot(whole, key_w, preferred_element_type=jnp.float32)
    value_low = jnp.dot(whole, value_w, preferred_element_type=jnp.float32).astype(jnp.bfloat16)
    q_unit, q_norm = head_unit(rope_apply(q_raw, cosine, sine, first_half), member)
    k_unit, k_norm = head_unit(rope_apply(k_raw, cosine, sine, first_half), member)
    query_low = (q_unit * qk_scale).astype(jnp.bfloat16)
    key_low = (k_unit * qk_scale).astype(jnp.bfloat16)
    query3 = query_low.reshape(shape3)
    key3 = key_low.reshape(shape3)
    value3 = value_low.reshape(shape3)
    attended, totals = attend(query3, key3, value3, block)
    attended_low = attended.reshape(length, width).astype(jnp.bfloat16)
    attn_sum = lax.psum_scatter(
        contract_cols(attended_low, out_w), "tensor", scatter_dimension=0, tiled=True
    )
    attn_unit, attn_norm = unit_rows(attn_sum)
    residual = tokens.astype(jnp.float32)
    mid, mid_norm = unit_rows(residual + alpha_attn * (attn_unit - residual))
    mid_low = mid.astype(jnp.bfloat16)
    up_w, gate_w, down_w = gather_feedforward(w_up, w_gate, w_down)
    mid_whole = lax.all_gather(mid_low, "tensor", axis=0, tiled=True)
    up_sum = jnp.dot(mid_whole, up_w, preferred_element_type=jnp.float32)
    gate_sum = jnp.dot(mid_whole, gate_w, preferred_element_type=jnp.float32)
    up_val = up_sum * up_scale
    gate_val = gate_sum * gate_scale
    sigma = jax.nn.sigmoid(gate_val)
    hidden_low = (up_val * (gate_val * sigma)).astype(jnp.bfloat16)
    mlp_sum = lax.psum_scatter(
        contract_cols(hidden_low, down_w), "tensor", scatter_dimension=0, tiled=True
    )
    mlp_unit, mlp_norm = unit_rows(mlp_sum)
    final, final_norm = unit_rows(mid + alpha_mlp * (mlp_unit - mid))
    output = final.astype(jnp.bfloat16)
    g_second = unit_back(cotangent.astype(jnp.float32), final, final_norm)
    g_alpha_mlp = jnp.sum((mlp_unit - mid) * g_second, axis=0)
    g_mlp_low = unit_back(alpha_mlp * g_second, mlp_unit, mlp_norm).astype(jnp.bfloat16)
    up_w, gate_w, down_w = gather_feedforward(w_up, w_gate, w_down)
    g_mlp_whole = lax.all_gather(g_mlp_low, "tensor", axis=0, tiled=True)
    down_grad = contract_rows(g_mlp_whole, hidden_low)
    g_hidden = jnp.dot(g_mlp_whole, down_w, preferred_element_type=jnp.float32)
    g_up = g_hidden * (gate_val * sigma)
    g_gate = g_hidden * up_val * (sigma * (1.0 + gate_val * (1.0 - sigma)))
    up_scale_grad = jnp.sum(g_up * up_sum, axis=0)
    gate_scale_grad = jnp.sum(g_gate * gate_sum, axis=0)
    g_up_low = (g_up * up_scale).astype(jnp.bfloat16)
    g_gate_low = (g_gate * gate_scale).astype(jnp.bfloat16)
    up_grad = contract_rows(mid_whole, g_up_low)
    gate_grad = contract_rows(mid_whole, g_gate_low)
    g_mid_part = contract_cols(g_up_low, up_w) + contract_cols(g_gate_low, gate_w)
    g_mid = (1.0 - alpha_mlp) * g_second + lax.psum_scatter(
        g_mid_part, "tensor", scatter_dimension=0, tiled=True
    )
    up_grad, gate_grad, down_grad = (
        lax.psum_scatter(up_grad, "dp", scatter_dimension=0, tiled=True),
        lax.psum_scatter(gate_grad, "dp", scatter_dimension=0, tiled=True),
        lax.psum_scatter(down_grad, "dp", scatter_dimension=0, tiled=True),
    )
    g_first = unit_back(g_mid, mid, mid_norm)
    g_alpha_attn = jnp.sum((attn_unit - residual) * g_first, axis=0)
    g_attn_low = unit_back(alpha_attn * g_first, attn_unit, attn_norm).astype(jnp.bfloat16)
    query_w, key_w, value_w, out_w = gather_attention(w_query, w_key, w_value, w_out)
    g_attn_whole = lax.all_gather(g_attn_low, "tensor", axis=0, tiled=True)
    out_grad = contract_rows(g_attn_whole, attended_low)
    g_attended_low = jnp.dot(g_attn_whole, out_w, preferred_element_type=jnp.float32).astype(
        jnp.bfloat16
    )
    g_query3, g_key3, g_value3 = attend_back(
        query3, key3, value3, g_attended_low.reshape(shape3), totals, block
    )
    g_query = g_query3.reshape(length, width)
    g_key = g_key3.reshape(length, width)
    qk_grad = jnp.sum(g_query * q_unit, axis=0) + jnp.sum(g_key * k_unit, axis=0)
    g_q_raw_low = rope_back(
        head_back(g_query * qk_scale, q_unit, q_norm, member), cosine, sine, first_half
    ).astype(jnp.bfloat16)
    g_k_raw_low = rope_back(
        head_back(g_key * qk_scale, k_unit, k_norm, member), cosine, sine, first_half
    ).astype(jnp.bfloat16)
    g_value_low = g_value3.reshape(length, width).astype(jnp.bfloat16)
    query_grad = contract_rows(whole, g_q_raw_low)
    key_grad = contract_rows(whole, g_k_raw_low)
    value_grad = contract_rows(whole, g_value_low)
    g_tok_part = (
        contract_cols(g_q_raw_low, query_w)
        + contract_cols(g_k_raw_low, key_w)
        + contract_cols(g_value_low, value_w)
    )
    tokens_grad = (1.0 - alpha_attn) * g_first + lax.psum_scatter(
        g_tok_part.astype(jnp.bfloat16), "tensor", scatter_dimension=0, tiled=True
    ).astype(jnp.float32)
    query_grad, key_grad, value_grad, out_grad = (
        lax.psum_scatter(query_grad, "dp", scatter_dimension=0, tiled=True),
        lax.psum_scatter(key_grad, "dp", scatter_dimension=0, tiled=True),
        lax.psum_scatter(value_grad, "dp", scatter_dimension=0, tiled=True),
        lax.psum_scatter(out_grad, "dp", scatter_dimension=0, tiled=True),
    )
    qk_grad, up_scale_grad, gate_scale_grad = lax.psum(
        (qk_grad, up_scale_grad, gate_scale_grad), "dp"
    )
    g_alpha_attn, g_alpha_mlp = lax.psum((g_alpha_attn, g_alpha_mlp), ("dp", "tensor"))
    return (
        output,
        tokens_grad,
        query_grad,
        key_grad,
        value_grad,
        out_grad,
        up_grad,
        gate_grad,
        down_grad,
        qk_grad,
        up_scale_grad,
        gate_scale_grad,
        g_alpha_attn,
        g_alpha_mlp,
    )


def solution(mesh):
    in_specs = (
        P(("dp", "tensor"), None),
        P("dp", "tensor"),
        P("dp", "tensor"),
        P("dp", "tensor"),
        P("dp", "tensor"),
        P("dp", "tensor"),
        P("dp", "tensor"),
        P("dp", "tensor"),
        P("tensor"),
        P("tensor"),
        P("tensor"),
        P(),
        P(),
        P(("dp", "tensor"), None),
    )
    out_specs = (
        P(("dp", "tensor"), None),
        P(("dp", "tensor"), None),
        P("dp", "tensor"),
        P("dp", "tensor"),
        P("dp", "tensor"),
        P("dp", "tensor"),
        P("dp", "tensor"),
        P("dp", "tensor"),
        P("dp", "tensor"),
        P("tensor"),
        P("tensor"),
        P("tensor"),
        P(),
        P(),
    )
    return jax.shard_map(
        on_device, mesh=mesh, in_specs=in_specs, out_specs=out_specs, check_vma=False
    )
```

profile of v0, /device:TPU:0, one launch (start us, length us, event | category | flops | bytes accessed | tf_op | source)
XLA Modules:
  0.0 1157.3 jit_solution(15452497443347139287)
XLA Ops:
  9.0 12.8 %all_gather.41 = bf16[1280,320]{1,0:T(8,128)(2,1)S(1)} all-gather(bf16[160,320]{1,0:T(8,128)(2,1)} %param.29), channel_id=1, replica_groups=mesh['dp'=8,'tensor'=4] {'dp'}, dimensions={0}, use_global_device_ids=true | all-gather | bytes 921600 | tf_op jit(solution)/shard_map/all_gather | solution.py:158
  21.8 11.6 %all_gather.43 = bf16[1280,320]{1,0:T(8,128)(2,1)} all-gather(bf16[160,320]{1,0:T(8,128)(2,1)S(1)} %copy-done.50), channel_id=1, replica_groups=mesh['dp'=8,'tensor'=4] {'dp'}, dimensions={0}, use_global_device_ids=true | all-gather | bytes 921600 | tf_op jit(solution)/shard_map/all_gather | solution.py:157
  33.3 11.4 all_gather.42
  44.7 11.5 all_gather.44
  56.6 11.3 all-gather.8.cloned.1.call-done
  67.9 3.0 fusion.124
  74.3 6.5 fusion.20
  80.9 1.6 fusion.55
  83.3 1.6 fusion.49
  84.9 2.5 multiply_convert_fusion.7
  87.5 2.0 fusion
  89.5 3.1 exponential_reduce_fusion
  96.0 2.9 fusion.67
  101.9 3.9 fusion.125
  106.4 92.1 %reduce-scatter.18.cloned.1.call-done = f32[256,1280]{1,0:T(8,128)} async-done(((f32[1024,1280]{1,0:T(8,128)}), f32[256,1280]{1,0:T(8,128)}) %reduce-scatter.18.cloned.1.call-update) | async-done | bytes 1310736 | tf_op jit(solution)/shard_map/reduce_scatter | solution.py:206
  198.5 1.6 multiply_reduce_fusion.14
  204.5 53.4 %all-gather.10.cloned.1.call-done = bf16[1024,1280]{1,0:T(8,128)(2,1)} async-done(((bf16[256,1280]{1,0:T(8,128)(2,1)}), bf16[1024,1280]{1,0:T(8,128)(2,1)}) %all-gather.10.cloned.1.call-update) | async-done | bytes 2621456 | tf_op jit(solution)/shard_map/all_gather | solution.py:214
  257.8 8.6 fusion.126
  266.4 24.5 %all-gather.12.cloned.1.call-done = bf16[1280,1280]{1,0:T(8,128)(2,1)} async-done(((bf16[160,1280]{1,0:T(8,128)(2,1)}), bf16[1280,1280]{1,0:T(8,128)(2,1)}) %all-gather.12.cloned.1.call-update) | async-done | bytes 3276816 | tf_op jit(solution)/shard_map/all_gather | solution.py:165
  290.8 11.3 multiply_convert_fusion.4
  302.1 23.2 %all-gather.16.cloned.1.call-done = bf16[1280,1280]{1,0:T(8,128)(2,1)} async-done(((bf16[160,1280]{1,0:T(8,128)(2,1)}), bf16[1280,1280]{1,0:T(8,128)(2,1)}) %all-gather.16.cloned.1.call-update) | async-done | bytes 3276816 | tf_op jit(solution)/shard_map/all_gather | solution.py:167
  325.4 8.7 fusion.127
  334.1 93.9 %reduce-scatter.20.cloned.1.call-done = f32[256,1280]{1,0:T(8,128)} async-done(((f32[1024,1280]{1,0:T(8,128)}), f32[256,1280]{1,0:T(8,128)}) %reduce-scatter.20.cloned.1.call-update) | async-done | bytes 1310736 | tf_op jit(solution)/shard_map/reduce_scatter | solution.py:221
  428.0 1.6 multiply_reduce_fusion.12
  435.4 54.5 %all-gather.18.cloned.1.call-done = bf16[1024,1280]{1,0:T(8,128)(2,1)} async-done(((bf16[256,1280]{1,0:T(8,128)(2,1)}), bf16[1024,1280]{1,0:T(8,128)(2,1)}) %all-gather.18.cloned.1.call-update) | async-done | bytes 2621456 | tf_op jit(solution)/shard_map/all_gather | solution.py:231
  490.0 11.1 multiply_reduce_fusion.1
  501.1 3.6 fusion.128
  505.5 5.4 convolution_add_fusion
  511.0 92.5 %reduce-scatter.22.cloned.1.call-done = f32[256,1280]{1,0:T(8,128)} async-done(((f32[1024,1280]{1,0:T(8,128)}), f32[256,1280]{1,0:T(8,128)}) %reduce-scatter.22.cloned.1.call-update) | async-done | bytes 1310736 | tf_op jit(solution)/shard_map/reduce_scatter | solution.py:243
  603.5 2.2 multiply_reduce_fusion.9
  606.1 2.2 multiply_reduce_fusion.5
  610.8 54.8 %all-gather.20.cloned.1.call-done = bf16[1024,1280]{1,0:T(8,128)(2,1)} async-done(((bf16[256,1280]{1,0:T(8,128)(2,1)}), bf16[1024,1280]{1,0:T(8,128)(2,1)}) %all-gather.20.cloned.1.call-update) | async-done | bytes 2621456 | tf_op jit(solution)/shard_map/all_gather | solution.py:255
  665.6 2.8 convolution_convert_fusion
  669.1 4.5 multiply_reduce_fusion.3
  673.7 4.2 multiply_convert_fusion.1
  680.1 3.9 multiply_reduce_fusion
  683.9 3.3 multiply_convert_fusion
  687.2 1.7 fusion.39
  689.1 1.6 fusion.58
  693.6 1.6 fusion.61
  695.2 7.2 fusion.35
  705.3 6.0 fusion.24
  714.6 3.0 fusion.12
  718.4 3.3 add_convert_fusion
  721.9 8.9 fusion.132
  731.0 9.7 fusion.68
  740.8 8.8 fusion.133
  750.7 4.0 convolution_bitcast_fusion.2
  754.7 2.8 copy.46
  758.6 3.9 convolution_bitcast_fusion.1
  762.5 2.8 copy.48
  766.4 3.9 convolution_bitcast_fusion
  770.3 2.8 copy.50
  774.2 4.6 fusion.131
  778.8 39.5 %all-reduce.2 = (f32[1280]{0:T(1024)}, f32[1280]{0:T(1024)}) all-reduce(f32[1280]{0:T(1024)S(1)} %get-tuple-element.110, f32[1280]{0:T(1024)S(1)} %get-tuple-element.108), channel_id=1, replica_groups=mesh['dp'=8,'tensor'=4] {'dp','tensor'}, use_global_device_ids=true, to_apply=%region_33.34 | all-reduce | flops 2560 | bytes 20480 | tf_op jit(solution)/shard_map/psum | solution.py:293
  818.3 1.6 multiply_reduce_fusion.7
  820.3 25.1 %all-reduce.3 = (f32[320]{0:T(512)}, f32[1280]{0:T(1024)}, f32[1280]{0:T(1024)}) all-reduce(f32[320]{0:T(512)S(1)} %add.253, f32[1280]{0:T(1024)S(1)} %get-tuple-element.107, f32[1280]{0:T(1024)S(1)} %get-tuple-element.106), channel_id=1, replica_groups=mesh['dp'=8,'tensor'=4] {'dp'}, use_global_device_ids=true, to_apply=%region_27.28 | all-reduce | flops 2880 | bytes 23040 | tf_op jit(solution)/shard_map/psum | solution.py:290
  845.4 2.3 convert_add_fusion.1
  847.7 59.1 %reduce-scatter.30.cloned.1.call-done = f32[160,1280]{1,0:T(8,128)} async-done(((f32[1280,1280]{1,0:T(8,128)}), f32[160,1280]{1,0:T(8,128)}) %reduce-scatter.30.cloned.1.call-update) | async-done | bytes 819216 | tf_op jit(solution)/shard_map/reduce_scatter | solution.py:248
  906.8 66.9 %reduce-scatter.32.cloned.1.call-done = f32[160,1280]{1,0:T(8,128)} async-done(((f32[1280,1280]{1,0:T(8,128)}), f32[160,1280]{1,0:T(8,128)}) %reduce-scatter.32.cloned.1.call-update) | async-done | bytes 819216 | tf_op jit(solution)/shard_map/reduce_scatter | solution.py:249
  973.7 43.9 %reduce-scatter.34.cloned.1.call-done = f32[160,320]{1,0:T(8,128)} async-done(((f32[1280,320]{1,0:T(8,128)}), f32[160,320]{1,0:T(8,128)}) %reduce-scatter.34.cloned.1.call-update) | async-done | bytes 204816
  1017.6 44.1 %reduce-scatter.36.cloned.1.call-done = f32[160,320]{1,0:T(8,128)} async-done(((f32[1280,320]{1,0:T(8,128)}), f32[160,320]{1,0:T(8,128)}) %reduce-scatter.36.cloned.1.call-update) | async-done | bytes 204816
  1061.7 43.9 %reduce-scatter.38.cloned.1.call-done = f32[160,320]{1,0:T(8,128)} async-done(((f32[1280,320]{1,0:T(8,128)}), f32[160,320]{1,0:T(8,128)}) %reduce-scatter.38.cloned.1.call-update) | async-done | bytes 204816
  1105.6 44.1 %reduce-scatter.26.cloned.1.call-done = f32[160,320]{1,0:T(8,128)} async-done(((f32[1280,320]{1,0:T(8,128)}), f32[160,320]{1,0:T(8,128)}) %reduce-scatter.26.cloned.1.call-update) | async-done | bytes 204816 | tf_op jit(solution)/shard_map/reduce_scatter | solution.py:288
  (228 shorter events, 43.8 us)
Async XLA Ops:
  8.0 13.7 %copy-start.50 = (bf16[160,320]{1,0:T(8,128)(2,1)S(1)}, bf16[160,320]{1,0:T(8,128)(2,1)}, u32[]{:S(2)}) copy-start(bf16[160,320]{1,0:T(8,128)(2,1)} %param.28) | copy-start | bytes 307204
  8.0 25.3 %copy-start.51 = (bf16[160,320]{1,0:T(8,128)(2,1)S(1)}, bf16[160,320]{1,0:T(8,128)(2,1)}, u32[]{:S(2)}) copy-start(bf16[160,320]{1,0:T(8,128)(2,1)} %param.27) | copy-start | bytes 307204
  8.0 59.9 %all-gather.8.cloned.1.call-start = ((), (), s32[]{:S(2)}) async-start(), calls=%async_computation.11 | async-start | bytes 3276800 | tf_op jit(solution)/shard_map/all_gather | solution.py:188
  8.8 189.7 %reduce-scatter.18.cloned.1.call-start = ((), (), s32[]{:S(2)}) async-start(), calls=%async_computation.12 | async-start | bytes 6553600 | tf_op jit(solution)/shard_map/reduce_scatter | solution.py:206
  9.0 35.8 %copy-start.52 = (bf16[160,320]{1,0:T(8,128)(2,1)S(1)}, bf16[160,320]{1,0:T(8,128)(2,1)}, u32[]{:S(2)}) copy-start(bf16[160,320]{1,0:T(8,128)(2,1)} %param.30) | copy-start | bytes 307204
  21.8 70.9 %copy-start.24 = (bf16[1280,320]{1,0:T(8,128)(2,1)}, bf16[1280,320]{1,0:T(8,128)(2,1)S(1)}, u32[]{:S(2)}) copy-start(bf16[1280,320]{1,0:T(8,128)(2,1)S(1)} %all_gather.41) | copy-start | bytes 2457604
  71.0 2.0 copy-start.56
  82.5 2.4 copy-start.53
  83.3 4.2 copy-start.10
  87.4 2.1 copy-start.14
  87.5 2.0 copy-start.31
  87.5 6.3 copy-start.33
  87.5 6.3 copy-start.35
  89.5 6.5 copy-start
  93.7 2.3 copy-start.38
  93.8 5.1 copy-start.42
  94.9 4.1 copy-start.1
  105.8 94.3 %copy-start.49 = (f32[1280]{0:T(1024)S(1)}, f32[1280]{0:T(1024)}, u32[]{:S(2)}) copy-start(f32[1280]{0:T(1024)} %param.37) | copy-start | bytes 15364
  105.8 98.7 %all-gather.14.cloned.1.call-start = ((), (), s32[]{:S(2)}) async-start(), calls=%async_computation.15 | async-start | bytes 3686400 | tf_op jit(solution)/shard_map/all_gather | solution.py:166
  106.4 151.4 %all-gather.10.cloned.1.call-start = ((), (), s32[]{:S(2)}) async-start(), calls=%async_computation.13 | async-start | bytes 3276800 | tf_op jit(solution)/shard_map/all_gather | solution.py:214
  198.5 1.7 copy-start.6
  202.8 88.0 %all-gather.12.cloned.1.call-start = ((), (), s32[]{:S(2)}) async-start(), calls=%async_computation.14 | async-start | bytes 3686400 | tf_op jit(solution)/shard_map/all_gather | solution.py:165
  203.4 122.0 %all-gather.16.cloned.1.call-start = ((), (), s32[]{:S(2)}) async-start(), calls=%async_computation.16 | async-start | bytes 3686400 | tf_op jit(solution)/shard_map/all_gather | solution.py:167
  204.1 86.7 %copy-start.57 = (f32[1280]{0:T(1024)S(1)}, f32[1280]{0:T(1024)}, u32[]{:S(2)}) copy-start(f32[1280]{0:T(1024)} %param.35) | copy-start | bytes 15364
  204.1 86.7 %copy-start.58 = (f32[1280]{0:T(1024)S(1)}, f32[1280]{0:T(1024)}, u32[]{:S(2)}) copy-start(f32[1280]{0:T(1024)} %param.36) | copy-start | bytes 15364
  204.1 223.9 %reduce-scatter.20.cloned.1.call-start = ((), (), s32[]{:S(2)}) async-start(), calls=%async_computation.17 | async-start | bytes 6553600 | tf_op jit(solution)/shard_map/reduce_scatter | solution.py:221
  334.1 95.6 %copy-start.48 = (f32[1280]{0:T(1024)S(1)}, f32[1280]{0:T(1024)}, u32[]{:S(2)}) copy-start(f32[1280]{0:T(1024)} %param.38) | copy-start | bytes 15364
  334.1 155.9 %all-gather.18.cloned.1.call-start = ((), (), s32[]{:S(2)}) async-start(), calls=%async_computation.18 | async-start | bytes 3276800 | tf_op jit(solution)/shard_map/all_gather | solution.py:231
  428.0 1.7 copy-start.2
  434.9 168.5 %reduce-scatter.22.cloned.1.call-start = ((), (), s32[]{:S(2)}) async-start(), calls=%async_computation.19 | async-start | bytes 6553600 | tf_op jit(solution)/shard_map/reduce_scatter | solution.py:243
  490.0 11.1 copy-start.55
  501.1 3.6 copy-start.60
  501.1 3.8 copy-start.59
  501.1 4.4 copy-start.54
  510.9 154.7 %all-gather.20.cloned.1.call-start = ((), (), s32[]{:S(2)}) async-start(), calls=%async_computation.20 | async-start | bytes 3276800 | tf_op jit(solution)/shard_map/all_gather | solution.py:255
  603.5 2.2 copy-start.7
  603.5 2.5 copy-start.9
  603.5 2.7 copy-start.16
  609.4 56.2 %copy-start.30 = (bf16[1280,320]{1,0:T(8,128)(2,1)S(1)}, bf16[1280,320]{1,0:T(8,128)(2,1)}, u32[]{:S(2)}) copy-start(bf16[1280,320]{1,0:T(8,128)(2,1)} %all_gather.44) | copy-start | bytes 2457604
  610.5 58.6 %copy-start.43 = (bf16[512,320]{0,1:T(8,128)(2,1)S(1)}, bf16[512,320]{0,1:T(8,128)(2,1)}, u32[]{:S(2)}) copy-start(bf16[512,320]{0,1:T(8,128)(2,1)} %copy-done.42) | copy-start | bytes 983044
  610.5 234.9 %reduce-scatter.24.cloned.1.call-start = ((), (), s32[]{:S(2)}) async-start(), calls=%async_computation.21 | async-start | bytes 3276800 | tf_op jit(solution)/shard_map/reduce_scatter | solution.py:281
  669.1 4.5 copy-start.40
  669.1 10.7 slice-start
  669.1 10.7 slice-start.1
  673.7 4.2 copy-start.36
  673.7 6.1 slice-start.2
  683.9 3.3 copy-start.15
  689.1 3.1 copy-start.3
  689.1 1.8 copy-start.11
  693.3 1.9 copy-start.17
  695.2 7.7 slice-start.3
  705.3 6.0 copy-start.28
  711.3 1.6 copy-start.22
  711.3 1.7 copy-start.26
  714.6 3.9 copy-start.25
  721.8 125.9 %reduce-scatter.28.cloned.1.call-start = ((), (), s32[]{:S(2)}) async-start(), calls=%async_computation.23 | async-start | bytes 7372800 | tf_op jit(solution)/shard_map/reduce_scatter | solution.py:247
  730.8 176.0 %reduce-scatter.30.cloned.1.call-start = ((), (), s32[]{:S(2)}) async-start(), calls=%async_computation.24 | async-start | bytes 7372800 | tf_op jit(solution)/shard_map/reduce_scatter | solution.py:248
  740.7 233.0 %reduce-scatter.32.cloned.1.call-start = ((), (), s32[]{:S(2)}) async-start(), calls=%async_computation.25 | async-start | bytes 7372800 | tf_op jit(solution)/shard_map/reduce_scatter | solution.py:249
  749.6 268.0 %reduce-scatter.34.cloned.1.call-start = ((), (), s32[]{:S(2)}) async-start(), calls=%async_computation.26 | async-start | bytes 2211840
  757.5 304.2 %reduce-scatter.36.cloned.1.call-start = ((), (), s32[]{:S(2)}) async-start(), calls=%async_computation.27 | async-start | bytes 2211840
  765.3 340.3 %reduce-scatter.38.cloned.1.call-start = ((), (), s32[]{:S(2)}) async-start(), calls=%async_computation.28 | async-start | bytes 2211840
  773.1 376.6 %reduce-scatter.26.cloned.1.call-start = ((), (), s32[]{:S(2)}) async-start(), calls=%async_computation.22 | async-start | bytes 2211840 | tf_op jit(solution)/shard_map/reduce_scatter | solution.py:288
  818.3 1.7 copy-start.5
  820.0 25.4 %copy-start.13 = (f32[256,1280]{1,0:T(8,128)S(1)}, f32[256,1280]{1,0:T(8,128)}, u32[]{:S(2)}) copy-start(f32[256,1280]{1,0:T(8,128)} %copy-done.12) | copy-start | bytes 3932164
  (20 other events, 23.4 us)
Sparse Core Ops, SparseCore 0:
  10.4 57.4 all-gather.7
  105.9 92.5 reduce-scatter.17
  334.2 93.7 reduce-scatter.19
  511.0 92.3 reduce-scatter.21
Sparse Core Ops, SparseCore 1:
  108.2 31.4 all-gather.13
  202.9 54.9 all-gather.9
  259.6 31.2 all-gather.11
  292.7 32.6 all-gather.15
  435.0 54.9 all-gather.17
  610.6 54.9 all-gather.19
  721.9 50.8 reduce-scatter.23
  776.6 63.3 reduce-scatter.27
  843.9 62.9 reduce-scatter.29
  910.8 62.8 reduce-scatter.31
  977.6 40.0 reduce-scatter.33
  1021.6 40.0 reduce-scatter.35
  1065.6 40.0 reduce-scatter.37
  1109.6 40.0 reduce-scatter.25
where the time goes:
time: 1160 us
  waiting for transfers between devices  805 us (69%)
  matrix products  153 us (13%)
  blocking collectives  112 us (10%)
  other arithmetic  43.9 us (4%)
  local copies, waits for them, and re-layouts  24.4 us (2%)
  between operations  16.9 us (1%)
    unnamed x21, waiting for transfers between devices  135 us
    reduce_scatter x1, waiting for transfers between devices, on_device(): lax.psum_scatter(contract_cols(hidden_low, down_w), 'tensor', scatter_dim...  93.9 us
    reduce_scatter x1, waiting for transfers between devices, on_device(): lax.psum_scatter(g_mid_part, 'tensor', scatter_dimension=0, tiled=True)  92.5 us
    reduce_scatter x1, waiting for transfers between devices, on_device(): lax.psum_scatter(contract_cols(attended_low, out_w), 'tensor', scatter_di...  92.1 us
    reduce_scatter x1, waiting for transfers between devices, on_device(): lax.psum_scatter(down_grad, 'dp', scatter_dimension=0, tiled=True)  66.9 us
    reduce_scatter x1, waiting for transfers between devices, on_device(): lax.psum_scatter(gate_grad, 'dp', scatter_dimension=0, tiled=True)  59.1 us
    all_gather x1, waiting for transfers between devices, on_device(): g_attn_whole = lax.all_gather(g_attn_low, 'tensor', axis=0, tiled=True)  54.8 us
    all_gather x1, waiting for transfers between devices, on_device(): g_mlp_whole = lax.all_gather(g_mlp_low, 'tensor', axis=0, tiled=True)  54.5 us
  transfers between devices with their start and end apart: 18, of which 15 were waited for; matrix products, arithmetic and copies ran while one was open for 7% of the time, Pallas kernels for 0%

commit v1 on v0

--- a/solution.py
+++ b/solution.py
@@ -161,8 +161,31 @@
 
 
 def gather_feedforward(w_up, w_gate, w_down):
+
+    def arrange_face_in(v0, on_dim):
+        u_next, passed, carry_out = (lax.axis_size("dp"), lax.axis_index("dp"), v0.shape[on_dim])
+        pile = list(map(lambda w: (w, (w + 1) % u_next), range(u_next)))
+        frames = list(map(lambda w: (w, (w - 1) % u_next), range(u_next)))
+        local_out = jnp.zeros(
+            (*v0.shape[:on_dim], u_next * carry_out, *v0.shape[on_dim + 1 :]), v0.dtype
+        )
+        local_out = lax.dynamic_update_slice_in_dim(local_out, v0, passed * carry_out, axis=on_dim)
+        w2 = u_next // 2
+        block_last = wide_out = v0
+        for pp in range(1, w2 + 1):
+            block_last = lax.ppermute(block_last, axis_name="dp", perm=pile)
+            local_out = lax.dynamic_update_slice_in_dim(
+                local_out, block_last, (passed - pp) % u_next * carry_out, axis=on_dim
+            )
+            if pp < u_next - w2:
+                wide_out = lax.ppermute(wide_out, axis_name="dp", perm=frames)
+                local_out = lax.dynamic_update_slice_in_dim(
+                    local_out, wide_out, (passed + pp) % u_next * carry_out, axis=on_dim
+                )
+        return local_out
+
     return (
-        lax.all_gather(w_up, "dp", axis=0, tiled=True),
+        arrange_face_in(w_up, 0),
         lax.all_gather(w_gate, "dp", axis=0, tiled=True),
         lax.all_gather(w_down, "dp", axis=0, tiled=True),
     )

time: 1160 us -> 1130 us (0.974)
  waiting for transfers between devices: 805 us -> 758 us
    all_gather x1, waiting for transfers between devices: 53.4 us -> 10.2 us  [on_device(): mid_whole = lax.all_gather(mid_low, 'tensor', axis=0, tiled=True)]
    ppermute x0 -> x7, waiting for transfers between devices: none -> 25.7 us  [the longest x4 25.7 us: arrange_face_in(): block_last = lax.ppermute(block_last, axis_name='dp', perm=pile)]
    all_gather x1 -> x0, waiting for transfers between devices: 24.5 us -> none  [gather_feedforward(): lax.all_gather(w_up, 'dp', axis=0, tiled=True)]
    unnamed x21 -> x20, waiting for transfers between devices: 135 us -> 134 us
  transfers between devices with their start and end apart: 18 -> 24, of which waited for: 15 -> 18; matrix products, arithmetic and copies ran while one was open for 7% -> 8% of each run, Pallas kernels for 0% -> 0%
where the time goes in v1:
time: 1130 us
  waiting for transfers between devices  758 us (67%)
  matrix products  150 us (13%)
  blocking collectives  113 us (10%)
  other arithmetic  45.5 us (4%)
  local copies, waits for them, and re-layouts  32 us (3%)
  between operations  17.1 us (2%)
    unnamed x20, waiting for transfers between devices  134 us
    reduce_scatter x1, waiting for transfers between devices, on_device(): lax.psum_scatter(contract_cols(hidden_low, down_w), 'tensor', scatter_dim...  93.9 us
    reduce_scatter x1, waiting for transfers between devices, on_device(): lax.psum_scatter(g_mid_part, 'tensor', scatter_dimension=0, tiled=True)  92.4 us
    reduce_scatter x1, waiting for transfers between devices, on_device(): lax.psum_scatter(contract_cols(attended_low, out_w), 'tensor', scatter_di...  92.1 us
    reduce_scatter x1, waiting for transfers between devices, on_device(): lax.psum_scatter(down_grad, 'dp', scatter_dimension=0, tiled=True)  67 us
    reduce_scatter x1, waiting for transfers between devices, on_device(): lax.psum_scatter(gate_grad, 'dp', scatter_dimension=0, tiled=True)  62.4 us
    all_gather x1, waiting for transfers between devices, on_device(): g_attn_whole = lax.all_gather(g_attn_low, 'tensor', axis=0, tiled=True)  55.2 us
    all_gather x1, waiting for transfers between devices, on_device(): g_mlp_whole = lax.all_gather(g_mlp_low, 'tensor', axis=0, tiled=True)  54.5 us
  transfers between devices with their start and end apart: 24, of which 18 were waited for; matrix products, arithmetic and copies ran while one was open for 8% of the time, Pallas kernels for 0%

profile of v1, /device:TPU:0, one launch (start us, length us, event | category | flops | bytes accessed | tf_op | source)
XLA Modules:
  0.0 1125.6 jit_solution(6600747210393966046)
XLA Ops:
  9.0 12.7 %all_gather.37 = bf16[1280,320]{1,0:T(8,128)(2,1)S(1)} all-gather(bf16[160,320]{1,0:T(8,128)(2,1)} %param.29), channel_id=1, replica_groups=mesh['dp'=8,'tensor'=4] {'dp'}, dimensions={0}, use_global_device_ids=true | all-gather | bytes 921600 | tf_op jit(solution)/shard_map/all_gather | solution.py:158
  21.6 12.6 %all_gather.39 = bf16[1280,320]{1,0:T(8,128)(2,1)} all-gather(bf16[160,320]{1,0:T(8,128)(2,1)} %param.28), channel_id=1, replica_groups=mesh['dp'=8,'tensor'=4] {'dp'}, dimensions={0}, use_global_device_ids=true | all-gather | bytes 921600 | tf_op jit(solution)/shard_map/all_gather | solution.py:157
  34.2 11.5 %all_gather.38 = bf16[1280,320]{1,0:T(8,128)(2,1)} all-gather(bf16[160,320]{1,0:T(8,128)(2,1)S(1)} %copy-done.50), channel_id=1, replica_groups=mesh['dp'=8,'tensor'=4] {'dp'}, dimensions={0}, use_global_device_ids=true | all-gather | bytes 921600 | tf_op jit(solution)/shard_map/all_gather | solution.py:156
  45.7 11.3 %all_gather.40 = bf16[1280,320]{1,0:T(8,128)(2,1)} all-gather(bf16[160,320]{1,0:T(8,128)(2,1)S(1)} %copy-done.51), channel_id=1, replica_groups=mesh['dp'=8,'tensor'=4] {'dp'}, dimensions={0}, use_global_device_ids=true | all-gather | bytes 921600 | tf_op jit(solution)/shard_map/all_gather | solution.py:159
  57.4 10.5 all-gather.7.cloned.1.call-done
  67.9 3.0 fusion.125
  74.3 6.5 fusion.20
  84.9 2.5 multiply_convert_fusion.7
  87.5 2.0 fusion
  89.5 3.1 exponential_reduce_fusion
  96.0 2.9 fusion.67
  101.4 3.9 fusion.126
  105.9 92.1 %reduce-scatter.18.cloned.1.call-done = f32[256,1280]{1,0:T(8,128)} async-done(((f32[1024,1280]{1,0:T(8,128)}), f32[256,1280]{1,0:T(8,128)}) %reduce-scatter.18.cloned.1.call-update) | async-done | bytes 1310736 | tf_op jit(solution)/shard_map/reduce_scatter | solution.py:229
  199.5 1.9 multiply_reduce_fusion.13
  203.2 2.6 collective-permute-start.1
  208.5 5.9 collective-permute-done
  214.4 2.7 collective-permute-start.3
  220.6 5.4 collective-permute-done.2
  226.1 2.6 collective-permute-start.5
  230.3 7.8 collective-permute-done.4
  239.9 6.7 collective-permute-done.6
  247.3 10.2 all-gather.9.cloned.1.call-done
  257.5 6.4 fusion.127
  263.9 2.3 copy-done.59
  266.3 8.1 multiply_convert_fusion.4
  274.3 16.2 %all-gather.13.cloned.1.call-done = bf16[1280,1280]{1,0:T(8,128)(2,1)} async-done(((bf16[160,1280]{1,0:T(8,128)(2,1)}), bf16[1280,1280]{1,0:T(8,128)(2,1)}) %all-gather.13.cloned.1.call-update) | async-done | bytes 3276816 | tf_op jit(solution)/shard_map/all_gather | solution.py:190
  290.5 8.7 fusion.128
  299.3 93.9 %reduce-scatter.20.cloned.1.call-done = f32[256,1280]{1,0:T(8,128)} async-done(((f32[1024,1280]{1,0:T(8,128)}), f32[256,1280]{1,0:T(8,128)}) %reduce-scatter.20.cloned.1.call-update) | async-done | bytes 1310736 | tf_op jit(solution)/shard_map/reduce_scatter | solution.py:244
  401.3 54.5 %all-gather.15.cloned.1.call-done = bf16[1024,1280]{1,0:T(8,128)(2,1)} async-done(((bf16[256,1280]{1,0:T(8,128)(2,1)}), bf16[1024,1280]{1,0:T(8,128)(2,1)}) %all-gather.15.cloned.1.call-update) | async-done | bytes 2621456 | tf_op jit(solution)/shard_map/all_gather | solution.py:254
  455.8 11.1 multiply_reduce_fusion.1
  466.9 3.6 fusion.69
  470.5 7.3 convolution_add_fusion
  477.9 92.4 %reduce-scatter.22.cloned.1.call-done = f32[256,1280]{1,0:T(8,128)} async-done(((f32[1024,1280]{1,0:T(8,128)}), f32[256,1280]{1,0:T(8,128)}) %reduce-scatter.22.cloned.1.call-update) | async-done | bytes 1310736 | tf_op jit(solution)/shard_map/reduce_scatter | solution.py:266
  570.3 2.2 multiply_reduce_fusion.9
  572.9 2.2 multiply_reduce_fusion.5
  577.6 55.2 %all-gather.17.cloned.1.call-done = bf16[1024,1280]{1,0:T(8,128)(2,1)} async-done(((bf16[256,1280]{1,0:T(8,128)(2,1)}), bf16[1024,1280]{1,0:T(8,128)(2,1)}) %all-gather.17.cloned.1.call-update) | async-done | bytes 2621456 | tf_op jit(solution)/shard_map/all_gather | solution.py:278
  632.8 2.8 convolution_convert_fusion
  636.4 4.5 multiply_reduce_fusion.3
  640.9 4.2 multiply_convert_fusion.1
  647.3 3.9 multiply_reduce_fusion
  651.2 3.3 multiply_convert_fusion
  662.3 7.2 fusion.35
  672.4 6.0 fusion.24
  681.7 3.0 fusion.12
  685.5 3.3 add_convert_fusion
  688.9 8.8 fusion.132
  698.0 9.7 fusion.68
  707.8 8.8 fusion.133
  717.7 4.0 convolution_bitcast_fusion.2
  721.8 2.8 copy.46
  724.7 3.9 convolution_bitcast_fusion.1
  728.6 2.9 copy.48
  731.6 3.9 convolution_bitcast_fusion
  735.5 2.9 copy.50
  738.5 4.6 fusion.131
  743.1 39.7 %all-reduce.2 = (f32[1280]{0:T(1024)}, f32[1280]{0:T(1024)}) all-reduce(f32[1280]{0:T(1024)S(1)} %get-tuple-element.110, f32[1280]{0:T(1024)S(1)} %get-tuple-element.108), channel_id=1, replica_groups=mesh['dp'=8,'tensor'=4] {'dp','tensor'}, use_global_device_ids=true, to_apply=%region_33.34 | all-reduce | flops 2560 | bytes 20480 | tf_op jit(solution)/shard_map/psum | solution.py:316
  784.7 25.1 %all-reduce.3 = (f32[320]{0:T(512)}, f32[1280]{0:T(1024)}, f32[1280]{0:T(1024)}) all-reduce(f32[320]{0:T(512)S(1)} %add.348, f32[1280]{0:T(1024)S(1)} %get-tuple-element.107, f32[1280]{0:T(1024)S(1)} %get-tuple-element.106), channel_id=1, replica_groups=mesh['dp'=8,'tensor'=4] {'dp'}, use_global_device_ids=true, to_apply=%region_27.28 | all-reduce | flops 2880 | bytes 23040 | tf_op jit(solution)/shard_map/psum | solution.py:313
  809.8 2.3 convert_add_fusion.1
  812.1 62.4 %reduce-scatter.30.cloned.1.call-done = f32[160,1280]{1,0:T(8,128)} async-done(((f32[1280,1280]{1,0:T(8,128)}), f32[160,1280]{1,0:T(8,128)}) %reduce-scatter.30.cloned.1.call-update) | async-done | bytes 819216 | tf_op jit(solution)/shard_map/reduce_scatter | solution.py:271
  874.4 67.0 %reduce-scatter.32.cloned.1.call-done = f32[160,1280]{1,0:T(8,128)} async-done(((f32[1280,1280]{1,0:T(8,128)}), f32[160,1280]{1,0:T(8,128)}) %reduce-scatter.32.cloned.1.call-update) | async-done | bytes 819216 | tf_op jit(solution)/shard_map/reduce_scatter | solution.py:272
  941.5 44.2 %reduce-scatter.34.cloned.1.call-done = f32[160,320]{1,0:T(8,128)} async-done(((f32[1280,320]{1,0:T(8,128)}), f32[160,320]{1,0:T(8,128)}) %reduce-scatter.34.cloned.1.call-update) | async-done | bytes 204816
  985.6 44.0 %reduce-scatter.36.cloned.1.call-done = f32[160,320]{1,0:T(8,128)} async-done(((f32[1280,320]{1,0:T(8,128)}), f32[160,320]{1,0:T(8,128)}) %reduce-scatter.36.cloned.1.call-update) | async-done | bytes 204816
  1029.7 44.2 %reduce-scatter.38.cloned.1.call-done = f32[160,320]{1,0:T(8,128)} async-done(((f32[1280,320]{1,0:T(8,128)}), f32[160,320]{1,0:T(8,128)}) %reduce-scatter.38.cloned.1.call-update) | async-done | bytes 204816
  1073.8 44.0 %reduce-scatter.26.cloned.1.call-done = f32[160,320]{1,0:T(8,128)} async-done(((f32[1280,320]{1,0:T(8,128)}), f32[160,320]{1,0:T(8,128)}) %reduce-scatter.26.cloned.1.call-update) | async-done | bytes 204816 | tf_op jit(solution)/shard_map/reduce_scatter | solution.py:311
  (248 shorter events, 60.8 us)
Async XLA Ops:
  8.0 26.2 %copy-start.50 = (bf16[160,320]{1,0:T(8,128)(2,1)S(1)}, bf16[160,320]{1,0:T(8,128)(2,1)}, u32[]{:S(2)}) copy-start(bf16[160,320]{1,0:T(8,128)(2,1)} %param.27) | copy-start | bytes 307204
  8.0 37.7 %copy-start.51 = (bf16[160,320]{1,0:T(8,128)(2,1)S(1)}, bf16[160,320]{1,0:T(8,128)(2,1)}, u32[]{:S(2)}) copy-start(bf16[160,320]{1,0:T(8,128)(2,1)} %param.30) | copy-start | bytes 307204
  8.0 59.9 %all-gather.7.cloned.1.call-start = ((), (), s32[]{:S(2)}) async-start(), calls=%async_computation.11 | async-start | bytes 3276800 | tf_op jit(solution)/shard_map/all_gather | solution.py:211
  8.8 189.2 %reduce-scatter.18.cloned.1.call-start = ((), (), s32[]{:S(2)}) async-start(), calls=%async_computation.12 | async-start | bytes 6553600 | tf_op jit(solution)/shard_map/reduce_scatter | solution.py:229
  21.6 71.0 %copy-start.23 = (bf16[1280,320]{1,0:T(8,128)(2,1)}, bf16[1280,320]{1,0:T(8,128)(2,1)S(1)}, u32[]{:S(2)}) copy-start(bf16[1280,320]{1,0:T(8,128)(2,1)S(1)} %all_gather.37) | copy-start | bytes 2457604
  80.9 4.0 copy-start.52
  83.2 4.2 copy-start.9
  87.4 6.3 copy-start.32
  87.5 6.3 copy-start.34
  89.5 6.5 copy-start
  93.7 2.3 copy-start.37
  93.8 5.1 copy-start.41
  94.8 4.1 copy-start.1
  98.9 2.5 copy-start.28
  105.3 94.2 %copy-start.49 = (f32[1280]{0:T(1024)S(1)}, f32[1280]{0:T(1024)}, u32[]{:S(2)}) copy-start(f32[1280]{0:T(1024)} %param.37) | copy-start | bytes 15364
  105.3 142.0 %all-gather.11.cloned.1.call-start = ((), (), s32[]{:S(2)}) async-start(), calls=%async_computation.14 | async-start | bytes 3686400 | tf_op jit(solution)/shard_map/all_gather | solution.py:189
  105.9 151.6 %all-gather.9.cloned.1.call-start = ((), (), s32[]{:S(2)}) async-start(), calls=%async_computation.13 | async-start | bytes 3276800 | tf_op jit(solution)/shard_map/all_gather | solution.py:237
  202.5 88.0 %all-gather.13.cloned.1.call-start = ((), (), s32[]{:S(2)}) async-start(), calls=%async_computation.15 | async-start | bytes 3686400 | tf_op jit(solution)/shard_map/all_gather | solution.py:190
  203.1 190.1 %reduce-scatter.20.cloned.1.call-start = ((), (), s32[]{:S(2)}) async-start(), calls=%async_computation.16 | async-start | bytes 6553600 | tf_op jit(solution)/shard_map/reduce_scatter | solution.py:244
  203.1 11.2 collective-permute-start
  203.2 11.2 collective-permute-start.1
  214.4 11.7 %collective-permute-start.2 = (bf16[160,1280]{1,0:T(8,128)(2,1)}, bf16[160,1280]{1,0:T(8,128)(2,1)S(1)}, u32[]{:S(2)}, u32[]{:S(2)}) collective-permute-start(bf16[160,1280]{1,0:T(8,128)(2,1)} %collective-permute-done), channel_id=1, source_target_pairs={{0,4},{4,8},{8,12},{12,16},{16,20},{20,24},{24,28},{28,0},{1,5},{5... | collective-permute-start | bytes 1228808 | tf_op jit(solution)/shard_map/ppermute | solution.py:176
  214.4 11.7 %collective-permute-start.3 = (bf16[160,1280]{1,0:T(8,128)(2,1)}, bf16[160,1280]{1,0:T(8,128)(2,1)S(1)}, u32[]{:S(2)}, u32[]{:S(2)}) collective-permute-start(bf16[160,1280]{1,0:T(8,128)(2,1)} %collective-permute-done.1), channel_id=1, source_target_pairs={{0,28},{4,0},{8,4},{12,8},{16,12},{20,16},{24,20},{28,24},{1,29},{... | collective-permute-start | bytes 1228808 | tf_op jit(solution)/shard_map/ppermute | solution.py:181
  226.1 12.0 %collective-permute-start.4 = (bf16[160,1280]{1,0:T(8,128)(2,1)S(1)}, bf16[160,1280]{1,0:T(8,128)(2,1)S(1)}, u32[]{:S(2)}, u32[]{:S(2)}) collective-permute-start(bf16[160,1280]{1,0:T(8,128)(2,1)S(1)} %collective-permute-done.2), channel_id=1, source_target_pairs={{0,4},{4,8},{8,12},{12,16},{16,20},{20,24},{24,28},{28,0},{1,5},{5... | collective-permute-start | bytes 1228808 | tf_op jit(solution)/shard_map/ppermute | solution.py:176
  226.1 13.0 %collective-permute-start.5 = (bf16[160,1280]{1,0:T(8,128)(2,1)S(1)}, bf16[160,1280]{1,0:T(8,128)(2,1)S(1)}, u32[]{:S(2)}, u32[]{:S(2)}) collective-permute-start(bf16[160,1280]{1,0:T(8,128)(2,1)S(1)} %collective-permute-done.3), channel_id=1, source_target_pairs={{0,28},{4,0},{8,4},{12,8},{16,12},{20,16},{24,20},{28,24},{1,29},{... | collective-permute-start | bytes 1228808 | tf_op jit(solution)/shard_map/ppermute | solution.py:181
  238.0 8.5 collective-permute-start.6
  247.3 18.9 %copy-start.56 = (f32[1280]{0:T(1024)S(1)}, f32[1280]{0:T(1024)}, u32[]{:S(2)}) copy-start(f32[1280]{0:T(1024)} %param.35) | copy-start | bytes 15364
  247.3 18.9 %copy-start.57 = (f32[1280]{0:T(1024)S(1)}, f32[1280]{0:T(1024)}, u32[]{:S(2)}) copy-start(f32[1280]{0:T(1024)} %param.36) | copy-start | bytes 15364
  257.5 8.8 copy-start.55
  263.9 2.3 copy-start.59
  299.2 95.5 %copy-start.48 = (f32[1280]{0:T(1024)S(1)}, f32[1280]{0:T(1024)}, u32[]{:S(2)}) copy-start(f32[1280]{0:T(1024)} %param.38) | copy-start | bytes 15364
  299.2 156.6 %all-gather.15.cloned.1.call-start = ((), (), s32[]{:S(2)}) async-start(), calls=%async_computation.17 | async-start | bytes 3276800 | tf_op jit(solution)/shard_map/all_gather | solution.py:254
  393.2 3.5 copy-start.36
  400.8 169.5 %reduce-scatter.22.cloned.1.call-start = ((), (), s32[]{:S(2)}) async-start(), calls=%async_computation.18 | async-start | bytes 6553600 | tf_op jit(solution)/shard_map/reduce_scatter | solution.py:266
  455.8 11.1 copy-start.53
  466.9 3.6 copy-start.58
  466.9 3.6 copy-start.60
  477.9 154.9 %all-gather.17.cloned.1.call-start = ((), (), s32[]{:S(2)}) async-start(), calls=%async_computation.19 | async-start | bytes 3276800 | tf_op jit(solution)/shard_map/all_gather | solution.py:278
  570.3 2.5 copy-start.8
  570.3 2.7 copy-start.15
  575.1 57.6 %copy-start.29 = (bf16[1280,320]{1,0:T(8,128)(2,1)S(1)}, bf16[1280,320]{1,0:T(8,128)(2,1)}, u32[]{:S(2)}) copy-start(bf16[1280,320]{1,0:T(8,128)(2,1)} %all_gather.40) | copy-start | bytes 2457604
  577.4 59.0 %copy-start.42 = (bf16[512,320]{0,1:T(8,128)(2,1)S(1)}, bf16[512,320]{0,1:T(8,128)(2,1)}, u32[]{:S(2)}) copy-start(bf16[512,320]{0,1:T(8,128)(2,1)} %copy-done.41) | copy-start | bytes 983044
  577.4 232.4 %reduce-scatter.24.cloned.1.call-start = ((), (), s32[]{:S(2)}) async-start(), calls=%async_computation.20 | async-start | bytes 3276800 | tf_op jit(solution)/shard_map/reduce_scatter | solution.py:304
  636.4 4.5 copy-start.39
  636.4 10.7 slice-start
  636.4 10.7 slice-start.1
  640.9 4.2 copy-start.35
  640.9 6.1 slice-start.2
  651.2 3.3 copy-start.14
  656.3 3.0 copy-start.3
  662.3 7.7 slice-start.3
  672.4 6.0 copy-start.27
  681.7 3.8 copy-start.24
  688.9 123.2 %reduce-scatter.28.cloned.1.call-start = ((), (), s32[]{:S(2)}) async-start(), calls=%async_computation.22 | async-start | bytes 7372800 | tf_op jit(solution)/shard_map/reduce_scatter | solution.py:270
  697.8 176.6 %reduce-scatter.30.cloned.1.call-start = ((), (), s32[]{:S(2)}) async-start(), calls=%async_computation.23 | async-start | bytes 7372800 | tf_op jit(solution)/shard_map/reduce_scatter | solution.py:271
  707.8 233.7 %reduce-scatter.32.cloned.1.call-start = ((), (), s32[]{:S(2)}) async-start(), calls=%async_computation.24 | async-start | bytes 7372800 | tf_op jit(solution)/shard_map/reduce_scatter | solution.py:272
  716.7 269.0 %reduce-scatter.34.cloned.1.call-start = ((), (), s32[]{:S(2)}) async-start(), calls=%async_computation.25 | async-start | bytes 2211840
  721.8 2.9 copy-start.20
  724.6 305.0 %reduce-scatter.36.cloned.1.call-start = ((), (), s32[]{:S(2)}) async-start(), calls=%async_computation.26 | async-start | bytes 2211840
  728.6 3.0 copy-start.46
  731.5 342.3 %reduce-scatter.38.cloned.1.call-start = ((), (), s32[]{:S(2)}) async-start(), calls=%async_computation.27 | async-start | bytes 2211840
  735.5 3.0 copy-start.18
  738.4 379.5 %reduce-scatter.26.cloned.1.call-start = ((), (), s32[]{:S(2)}) async-start(), calls=%async_computation.21 | async-start | bytes 2211840 | tf_op jit(solution)/shard_map/reduce_scatter | solution.py:311
  784.5 25.3 %copy-start.12 = (f32[256,1280]{1,0:T(8,128)S(1)}, f32[256,1280]{1,0:T(8,128)}, u32[]{:S(2)}) copy-start(f32[256,1280]{1,0:T(8,128)} %copy-done.11) | copy-start | bytes 3932164
  (26 other events, 38.8 us)
Sparse Core Ops, SparseCore 0:
  10.4 57.4 all-gather.6
  105.4 92.5 reduce-scatter.17
  299.3 93.7 reduce-scatter.19
  577.5 55.2 all-gather.16
  689.0 51.0 reduce-scatter.23
  743.9 63.5 reduce-scatter.27
  811.5 62.8 reduce-scatter.29
  878.5 62.9 reduce-scatter.31
  945.5 40.1 reduce-scatter.33
  989.5 40.1 reduce-scatter.35
  1033.6 40.1 reduce-scatter.37
  1077.7 40.1 reduce-scatter.25
Sparse Core Ops, SparseCore 1:
  107.7 31.4 all-gather.10
  202.6 54.9 all-gather.8
  259.3 31.2 all-gather.12
  400.8 54.9 all-gather.14
  477.9 92.3 reduce-scatter.21
